TPU v7x, 32 devices: a whole 2x2x4 slice. The times are simulated.
32 devices in a mesh: seq: 8 (over y, x, core), head: 4 (over z).
Axes of the slice: x: 2, y: 2, z: 4, core: 2. Of those that a mesh axis runs over, the one named last changes fastest.
Arguments:
- latent: bfloat16 [8, 1024, 2048], P('seq', None, 'head'), may hold values from -6 to 6
- modulation: float32 [9, 2048], replicated, may hold values from -3 to 3
- spatial_qkv: bfloat16 [3, 2048, 2048], P(None, None, 'head')
- spatial_out: bfloat16 [2048, 2048], P('head'), may hold values from -0.125 to 0.125
- temporal_qkv: bfloat16 [3, 2048, 2048], P(None, None, 'head')
- temporal_out: bfloat16 [2048, 2048], P('head'), may hold values from -0.125 to 0.125
- hidden_weight: bfloat16 [2048, 8192], P(None, 'head'), may hold values from -0.125 to 0.125
- output_weight: bfloat16 [8192, 2048], P('head'), may hold values from -0.0625 to 0.0625
Outputs:
- block_out: bfloat16 [8, 1024, 2048], P(None, 'seq', 'head')
All inputs are finite; a program needn't handle non-finite values.
Results may differ from a plain program's by a relative error of at most 0.009.
Values may be sent and summed in bfloat16 or wider, within the bound.
No kernel may reach another device: no remote copies, remote signals or barrier semaphores. Data moves between devices by JAX's collectives and lax.ppermute only.
A program may use at most 128 MiB of HBM per device.

v0:
```python
import jax
import jax.numpy as jnp
from jax import lax
from jax.sharding import PartitionSpec as P

HD = 64


def layer_norm(values):
    average = jnp.mean(values, axis=-1, keepdims=True)
    centred = values - average
    variance = jnp.mean(centred * centred, axis=-1, keepdims=True)
    return centred * lax.rsqrt(variance + 1e-06)


def modulate(stream, modulation, offset):
    normed = layer_norm(stream.astype(jnp.float32))
    return (normed * (1.0 + modulation[offset + 1]) + modulation[offset]).astype(jnp.bfloat16)


def attend(query, keys, values):
    scores = jnp.einsum(
        "glhd,gmhd->ghlm", query, keys, preferred_element_type=jnp.float32
    ) * HD ** (-0.5)
    attn_weights = jax.nn.softmax(scores, axis=-1).astype(jnp.bfloat16)
    return jnp.einsum(
        "ghlm,gmhd->glhd", attn_weights, values, preferred_element_type=jnp.float32
    ).astype(jnp.bfloat16)


def project_three(normed, weights):
    return [
        jnp.dot(normed, weights[member], preferred_element_type=jnp.float32).astype(jnp.bfloat16)
        for member in range(3)
    ]


def column_adder(columns, portion):
    return jnp.dot(portion, columns, preferred_element_type=jnp.float32)


def per_device(
    latent,
    modulation,
    spatial_qkv,
    spatial_out,
    temporal_qkv,
    temporal_out,
    hidden_weight,
    output_weight,
):
    width_local = latent.shape[2]
    heads_local = width_local // HD
    anchor = lax.axis_index("head") * width_local
    local_rows = lax.dynamic_slice_in_dim(modulation, anchor, width_local, 1)
    full_spatial = lax.all_gather(latent, "head", axis=2, tiled=True)
    normed = modulate(full_spatial, modulation, 0)
    frames_local = latent.shape[0]
    patches = latent.shape[1]
    query, keys, values = [
        member.reshape(frames_local, patches, heads_local, HD)
        for member in project_three(normed, spatial_qkv)
    ]
    spatial = lax.map(
        lambda triple: attend(triple[0][None], triple[1][None], triple[2][None])[0],
        (query, keys, values),
    )
    spatial = spatial.reshape(frames_local, patches, width_local)
    columns = lax.all_to_all(spatial_out, "head", split_axis=1, concat_axis=0, tiled=True)
    reduced = column_adder(columns, lax.all_gather(spatial, "head", axis=2, tiled=True))
    stream_one = (latent.astype(jnp.float32) + local_rows[2] * reduced).astype(jnp.bfloat16)
    full_stream = lax.all_gather(stream_one, "head", axis=2, tiled=True)
    normed = modulate(full_stream, modulation, 3)
    stacked = jnp.stack(project_three(normed, temporal_qkv), axis=2)
    moved, stream_temporal = (
        lax.all_to_all(stacked, "seq", split_axis=1, concat_axis=0, tiled=True),
        lax.all_to_all(stream_one, "seq", split_axis=1, concat_axis=0, tiled=True),
    )
    query, keys, values = (moved[:, :, 0], moved[:, :, 1], moved[:, :, 2])
    frames = stream_temporal.shape[0]
    patches_local = stream_temporal.shape[1]

    def to_groups(tensor):
        return jnp.transpose(tensor.reshape(frames, patches_local, heads_local, HD), (1, 0, 2, 3))

    temporal = attend(to_groups(query), to_groups(keys), to_groups(values))
    temporal = jnp.transpose(temporal, (1, 0, 2, 3)).reshape(frames, patches_local, width_local)
    columns = lax.all_to_all(temporal_out, "head", split_axis=1, concat_axis=0, tiled=True)
    reduced = column_adder(columns, lax.all_gather(temporal, "head", axis=2, tiled=True))
    stream_two = (stream_temporal.astype(jnp.float32) + local_rows[5] * reduced).astype(
        jnp.bfloat16
    )
    full_two = lax.all_gather(stream_two, "head", axis=2, tiled=True)
    normed = modulate(full_two, modulation, 6)
    pre_act = jnp.dot(normed, hidden_weight, preferred_element_type=jnp.float32)
    hidden = jax.nn.gelu(pre_act, approximate=True).astype(jnp.bfloat16)
    partial_sums = jnp.dot(hidden, output_weight, preferred_element_type=jnp.float32)
    reduced = lax.psum_scatter(partial_sums, "head", scatter_dimension=2, tiled=True)
    return (stream_two.astype(jnp.float32) + local_rows[8] * reduced).astype(jnp.bfloat16)


def solution(mesh):
    in_specs = (
        P("seq", None, "head"),
        P(),
        P(None, None, "head"),
        P("head", None),
        P(None, None, "head"),
        P("head", None),
        P(None, "head"),
        P("head", None),
    )
    out_specs = P(None, "seq", "head")
    return jax.shard_map(
        per_device, mesh=mesh, in_specs=in_specs, out_specs=out_specs, check_vma=False
    )
```

profile of v0, /device:TPU:0, one launch (start us, length us, event | category | flops | bytes accessed | tf_op | source)
XLA Modules:
  0.0 838.2 jit_solution(230585978647317202)
XLA Ops:
  7.3 1.7 slice_add_fusion
  9.0 83.4 %all-gather.6.cloned.1.call-done = bf16[1,1024,2048]{2,1,0:T(8,128)(2,1)} async-done(((bf16[1,1024,512]{2,1,0:T(8,128)(2,1)}), bf16[1,1024,2048]{2,1,0:T(8,128)(2,1)}) %all-gather.6.cloned.1.call-update) | async-done | bytes 4194320 | tf_op jit(solution)/shard_map/all_gather | solution.py:56
  92.4 3.0 convert_reduce_fusion.2
  97.1 1.9 fusion.42
  99.0 2.4 fusion.95
  101.4 2.4 fusion.98
  103.8 2.4 fusion.101
  106.3 14.6 %fusion.131 = (f32[8,1024]{1,0:T(8,128)S(1)}, f32[8,1024,1024]{1,2,0:T(8,128)}) fusion(bf16[1024,8,64]{0,2,1:T(8,128)(2,1)S(1)} %bitcast.158, bf16[1024,8,64]{0,2,1:T(8,128)(2,1)S(1)} %bitcast.159), kind=kOutput, calls=%fused_computation.121 | convolution fusion | flops 1098908672 | bytes 35684352 | tf_op jit(solution)/shard_map/while/body/eval_jaxpr/sub | solution.py:25
  120.9 13.4 %fusion.113 = bf16[8,64,1024]{2,1,0:T(8,128)(2,1)} fusion(bf16[1024,8,64]{0,2,1:T(8,128)(2,1)S(1)} %bitcast.157, f32[8,1024,1024]{1,2,0:T(8,128)} %get-tuple-element.33, f32[8,1024]{1,0:T(8,128)S(1)} %get-tuple-element.32), kind=kOutput, calls=%fused_computation.100 | convolution fusion | flops 1091043328 | bytes 35684352 | tf_op jit(solution)/shard_map/while/body/eval_jaxpr/ghlm,gmhd->glhd/dot_general | solution.py:26
  134.3 2.5 copy.49
  136.8 3.8 all-to-all-start
  141.7 100.5 %all-to-all-done = bf16[512,4,512]{0,2,1:T(8,128)(2,1)S(1)} async-done(((bf16[512,4,512]{0,2,1:T(8,128)(2,1)}), bf16[512,4,512]{0,2,1:T(8,128)(2,1)S(1)}, u32[]{:S(2)}, u32[]{:S(2)}) %all-to-all-start) | async-done | bytes 2097184 | tf_op jit(solution)/shard_map/all_to_all | solution.py:69
  242.2 2.4 copy.50
  244.6 12.0 %all-gather.8.cloned.1.call-done = bf16[1,1024,2048]{1,2,0:T(8,128)(2,1)} async-done(((bf16[1,1024,512]{1,2,0:T(8,128)(2,1)}), bf16[1,1024,2048]{1,2,0:T(8,128)(2,1)}) %all-gather.8.cloned.1.call-update) | async-done | bytes 4194320 | tf_op jit(solution)/shard_map/all_gather | solution.py:70
  256.6 6.2 fusion.76
  262.9 79.9 %all-gather.10.cloned.1.call-done = bf16[1,1024,2048]{2,1,0:T(8,128)(2,1)} async-done(((bf16[1,1024,512]{2,1,0:T(8,128)(2,1)}), bf16[1,1024,2048]{2,1,0:T(8,128)(2,1)}) %all-gather.10.cloned.1.call-update) | async-done | bytes 4194320 | tf_op jit(solution)/shard_map/all_gather | solution.py:72
  342.8 3.0 convert_reduce_fusion.1
  347.5 1.9 fusion.43
  349.8 2.3 fusion.114
  352.1 2.3 fusion.117
  354.4 2.3 fusion.120
  357.1 2.7 copy.52
  359.8 52.9 %all_to_all.59 = bf16[1,1024,3,512]{3,2,0,1:T(4,128)(2,1)S(1)} all-to-all(bf16[1,1024,3,512]{3,2,0,1:T(4,128)(2,1)S(1)} %copy.52), channel_id=1, replica_groups=mesh['seq'=8,'head'=4] {'seq'}, dimensions={1} | all-to-all | bytes 6291456 | tf_op jit(solution)/shard_map/all_to_all | solution.py:76
  413.5 1.5 fusion.129
  415.7 3.0 copy.59
  418.7 1.6 copy.56
  420.3 3.8 copy.57
  424.1 2.8 fusion.66
  426.9 4.6 fusion.132
  432.2 3.0 copy.55
  435.2 4.2 convert_bitcast_fusion
  439.4 3.3 copy.61
  442.7 1.5 copy.62
  444.3 1.6 copy.71
  446.4 7.0 reduce.8
  453.5 1.6 reshape.197
  455.1 3.6 all-to-all-start.1
  458.6 1.6 copy.70
  460.2 13.7 %all-to-all-done.1 = bf16[8,2,32768]{2,1,0:T(2,128)(2,1)S(1)} async-done(((bf16[8,2,32768]{2,1,0:T(2,128)(2,1)}), bf16[8,2,32768]{2,1,0:T(2,128)(2,1)S(1)}, u32[]{:S(2)}, u32[]{:S(2)}) %all-to-all-start.1) | async-done | bytes 1048608 | tf_op jit(solution)/shard_map/all_to_all | solution.py:77
  473.9 4.4 all-to-all-start.3
  479.5 1.6 copy.66
  481.1 85.2 %all-to-all-done.3 = bf16[512,4,512]{2,0,1:T(8,128)(2,1)} async-done(((bf16[512,4,512]{2,0,1:T(8,128)(2,1)}), bf16[512,4,512]{2,0,1:T(8,128)(2,1)}, u32[]{:S(2)}, u32[]{:S(2)}) %all-to-all-start.3) | async-done | bytes 2097184 | tf_op jit(solution)/shard_map/all_to_all | solution.py:88
  566.2 6.7 add_convert_fusion.1
  573.3 79.0 %all-gather.14.cloned.1.call-done = bf16[8,128,2048]{2,1,0:T(8,128)(2,1)} async-done(((bf16[8,128,512]{2,1,0:T(8,128)(2,1)}), bf16[8,128,2048]{2,1,0:T(8,128)(2,1)}) %all-gather.14.cloned.1.call-update) | async-done | bytes 4194320 | tf_op jit(solution)/shard_map/all_gather | solution.py:93
  652.3 3.0 convert_reduce_fusion
  657.0 27.8 %fusion.33 = f32[8,128,2048]{2,1,0:T(8,128)} fusion(bf16[2048,2048]{1,0:T(8,128)(2,1)} %param.15, bf16[2048,2048]{1,0:T(8,128)(2,1)} %param.14, bf16[8,128,2048]{2,1,0:T(8,128)(2,1)} %all-gather.14.cloned.1.call-done, f32[2048]{0:T(1024)S(1)} %bitcast.150, f32[2048]{0:T(1024)S(1)} %bitcast.149, f32[8,128]{1,0:T(8,128)S(1)} %add_rsqrt_fusion, ...), kind=kOutput, calls=%fused_computation.41 | convolution fusion | flops 17211326464 | bytes 29384704 | tf_op jit(solution)/shard_map/dot_general | solution.py:97
  684.8 143.3 %reduce-scatter.2.cloned.1.call-done = f32[8,128,512]{2,1,0:T(8,128)} async-done(((f32[8,128,2048]{2,1,0:T(8,128)}), f32[8,128,512]{2,1,0:T(8,128)}) %reduce-scatter.2.cloned.1.call-update) | async-done | bytes 2097168 | tf_op jit(solution)/shard_map/reduce_scatter | solution.py:98
  828.1 2.9 add_convert_fusion
  (61 shorter events, 11.9 us)
Async XLA Ops:
  6.5 85.9 %all-gather.6.cloned.1.call-start = ((), (), s32[]{:S(2)}) async-start(), calls=%async_computation.5 | async-start | bytes 5242880 | tf_op jit(solution)/shard_map/all_gather | solution.py:56
  7.3 249.4 %all-gather.8.cloned.1.call-start = ((), (), s32[]{:S(2)}) async-start(), calls=%async_computation.6 | async-start | bytes 5242880 | tf_op jit(solution)/shard_map/all_gather | solution.py:70
  92.4 3.4 copy-start
  95.8 3.1 slice-start
  97.1 1.9 slice-start.1
  120.9 13.4 %copy-start.6 = (bf16[512,2048]{1,0:T(8,128)(2,1)S(1)}, bf16[512,2048]{1,0:T(8,128)(2,1)}, u32[]{:S(2)}) copy-start(bf16[512,2048]{1,0:T(8,128)(2,1)} %param.11) | copy-start | bytes 6291460
  136.8 119.8 %copy-start.8 = (bf16[1,1024,512]{2,1,0:T(8,128)(2,1)S(1)}, bf16[1,1024,512]{2,1,0:T(8,128)(2,1)}, u32[]{:S(2)}) copy-start(bf16[1,1024,512]{2,1,0:T(8,128)(2,1)} %param.8) | copy-start | bytes 3145732
  136.8 105.4 %all-to-all-start = ((bf16[512,4,512]{0,2,1:T(8,128)(2,1)}), bf16[512,4,512]{0,2,1:T(8,128)(2,1)S(1)}, u32[]{:S(2)}, u32[]{:S(2)}) async-start(bf16[512,4,512]{0,2,1:T(8,128)(2,1)} %bitcast.133), calls=%async_computation | async-start | bytes 4194304 | tf_op jit(solution)/shard_map/all_to_all | solution.py:69
  140.6 202.2 %all-gather.10.cloned.1.call-start = ((), (), s32[]{:S(2)}) async-start(), calls=%async_computation.7 | async-start | bytes 5242880 | tf_op jit(solution)/shard_map/all_gather | solution.py:72
  262.8 303.4 %all-gather.12.cloned.1.call-start = ((), (), s32[]{:S(2)}) async-start(), calls=%async_computation.8 | async-start | bytes 5242880 | tf_op jit(solution)/shard_map/all_gather | solution.py:89
  342.8 3.4 copy-start.1
  346.3 3.1 slice-start.2
  347.5 2.3 slice-start.3
  426.9 4.7 copy-start.5
  439.4 4.8 copy-start.3
  453.5 5.2 copy-start.7
  455.1 18.9 %all-to-all-start.1 = ((bf16[8,2,32768]{2,1,0:T(2,128)(2,1)}), bf16[8,2,32768]{2,1,0:T(2,128)(2,1)S(1)}, u32[]{:S(2)}, u32[]{:S(2)}) async-start(bf16[8,2,32768]{2,1,0:T(2,128)(2,1)} %reshape.197), calls=%async_computation.1 | async-start | bytes 2097152 | tf_op jit(solution)/shard_map/all_to_all | solution.py:77
  473.9 92.3 %all-to-all-start.3 = ((bf16[512,4,512]{2,0,1:T(8,128)(2,1)}), bf16[512,4,512]{2,0,1:T(8,128)(2,1)}, u32[]{:S(2)}, u32[]{:S(2)}) async-start(bf16[512,4,512]{2,0,1:T(8,128)(2,1)} %bitcast.129), calls=%async_computation.3 | async-start | bytes 4194304 | tf_op jit(solution)/shard_map/all_to_all | solution.py:88
  478.4 173.9 %all-gather.14.cloned.1.call-start = ((), (), s32[]{:S(2)}) async-start(), calls=%async_computation.9 | async-start | bytes 5242880 | tf_op jit(solution)/shard_map/all_gather | solution.py:93
  573.0 84.0 %copy-start.10 = (f32[1,2048]{1,0:T(1,128)S(1)}, f32[1,2048]{1,0:T(1,128)}, u32[]{:S(2)}) copy-start(f32[1,2048]{1,0:T(1,128)} %get-tuple-element.31) | copy-start | bytes 24580
  573.0 84.0 %copy-start.9 = (f32[1,2048]{1,0:T(1,128)S(1)}, f32[1,2048]{1,0:T(1,128)}, u32[]{:S(2)}) copy-start(f32[1,2048]{1,0:T(1,128)} %get-tuple-element.26) | copy-start | bytes 24580
  573.0 255.1 %reduce-scatter.2.cloned.1.call-start = ((), (), s32[]{:S(2)}) async-start(), calls=%async_computation.10 | async-start | bytes 10485760 | tf_op jit(solution)/shard_map/reduce_scatter | solution.py:98
  652.3 3.4 copy-start.2
  684.8 143.3 %copy-start.4 = (bf16[8,128,512]{2,1,0:T(8,128)(2,1)S(1)}, bf16[8,128,512]{2,1,0:T(8,128)(2,1)}, u32[]{:S(2)}) copy-start(bf16[8,128,512]{2,1,0:T(8,128)(2,1)} %add_convert_fusion.1) | copy-start | bytes 3145732
Sparse Core Ops, SparseCore 0:
  8.9 83.4 all-gather.5
  134.4 122.1 all-gather.7
  263.0 79.7 all-gather.9
  444.4 121.0 all-gather.11
  573.1 79.1 all-gather.13
  685.0 143.0 reduce-scatter.1
where the time goes:
time: 849 us; the launch traced here: 838 us
  waiting for transfers between devices  598 us (70%)
  matrix products  90 us (11%)
  blocking collectives  52.9 us (6%)
  local copies, waits for them, and re-layouts  38 us (4%)
  other arithmetic  33 us (4%)
  between operations  14.2 us (2%)
  starting transfers between devices  12.4 us (1%)
    reduce_scatter x1, waiting for transfers between devices, per_device(): lax.psum_scatter(partial_sums, 'head', scatter_dimension=2, tiled=True)  143 us
    all_to_all x1, waiting for transfers between devices, per_device(): lax.all_to_all(spatial_out, 'head', split_axis=1, concat_axis=0, tiled=True)  100 us
    all_to_all x1, waiting for transfers between devices, per_device(): lax.all_to_all(temporal_out, 'head', split_axis=1, concat_axis=0, tiled=T...  85.2 us
    all_gather x1, waiting for transfers between devices, per_device(): full_spatial = lax.all_gather(latent, 'head', axis=2, tiled=True)  83.4 us
    all_gather x1, waiting for transfers between devices, per_device(): full_stream = lax.all_gather(stream_one, 'head', axis=2, tiled=True)  79.9 us
    all_gather x1, waiting for transfers between devices, per_device(): full_two = lax.all_gather(stream_two, 'head', axis=2, tiled=True)  79 us
    all_to_all x1, blocking collectives, per_device(): lax.all_to_all(stacked, 'seq', split_axis=1, concat_axis=0, tiled=True)  52.9 us
    dot_general x1, matrix products, per_device(): jnp.dot(hidden, output_weight, preferred_element_type=jnp.float32)  27.8 us
  transfers between devices with their start and end apart: 9, of which 8 were waited for; matrix products, arithmetic and copies ran while one was open for 3% of the time, Pallas kernels for 0%

commit v1 on v0

--- a/solution.py
+++ b/solution.py
@@ -53,7 +53,7 @@
     heads_local = width_local // HD
     anchor = lax.axis_index("head") * width_local
     local_rows = lax.dynamic_slice_in_dim(modulation, anchor, width_local, 1)
-    full_spatial = lax.all_gather(latent, "head", axis=2, tiled=True)
+    full_spatial = jnp.concatenate(lax.all_gather(latent, "head"), axis=2)
     normed = modulate(full_spatial, modulation, 0)
     frames_local = latent.shape[0]
     patches = latent.shape[1]

time: 849 us -> 854 us (level)
  no operation moved by 1% of the time
where the time goes in v1:
time: 854 us; the launch traced here: 846 us
  waiting for transfers between devices  598 us (70%)
  matrix products  90.5 us (11%)
  blocking collectives  52.7 us (6%)
  local copies, waits for them, and re-layouts  44.9 us (5%)
  other arithmetic  33.7 us (4%)
  between operations  14 us (2%)
  starting transfers between devices  12.2 us (1%)
    reduce_scatter x1, waiting for transfers between devices, per_device(): lax.psum_scatter(partial_sums, 'head', scatter_dimension=2, tiled=True)  143 us
    all_to_all x1, waiting for transfers between devices, per_device(): lax.all_to_all(spatial_out, 'head', split_axis=1, concat_axis=0, tiled=True)  101 us
    all_to_all x1, waiting for transfers between devices, per_device(): lax.all_to_all(temporal_out, 'head', split_axis=1, concat_axis=0, tiled=T...  85.1 us
    all_gather x1, waiting for transfers between devices, per_device(): full_spatial = jnp.concatenate(lax.all_gather(latent, 'head'), axis=2)  83.3 us
    all_gather x1, waiting for transfers between devices, per_device(): full_stream = lax.all_gather(stream_one, 'head', axis=2, tiled=True)  79.9 us
    all_gather x1, waiting for transfers between devices, per_device(): full_two = lax.all_gather(stream_two, 'head', axis=2, tiled=True)  79.1 us
    all_to_all x1, blocking collectives, per_device(): lax.all_to_all(stacked, 'seq', split_axis=1, concat_axis=0, tiled=True)  52.7 us
    dot_general x1, matrix products, per_device(): jnp.dot(hidden, output_weight, preferred_element_type=jnp.float32)  27.8 us
  transfers between devices with their start and end apart: 9, of which 8 were waited for; matrix products, arithmetic and copies ran while one was open for 3% of the time, Pallas kernels for 0%

profile of v1, /device:TPU:0, one launch (start us, length us, event | category | flops | bytes accessed | tf_op | source)
XLA Modules:
  0.0 846.0 jit_solution(3585602246681475795)
XLA Ops:
  7.3 1.7 slice_add_fusion
  9.1 83.3 %all-gather.15.cloned.1.call-done = bf16[4,1024,512]{2,1,0:T(8,128)(2,1)} async-done(((bf16[1,1024,512]{2,1,0:T(8,128)(2,1)}), bf16[4,1024,512]{2,1,0:T(8,128)(2,1)}) %all-gather.15.cloned.1.call-update) | async-done | bytes 4194320 | tf_op jit(solution)/shard_map/all_gather | solution.py:56
  92.4 6.3 copy.51
  98.7 3.0 convert_reduce_fusion.2
  104.2 1.6 fusion.36
  106.3 2.4 fusion.94
  108.8 2.4 fusion.97
  111.2 2.4 fusion.100
  113.7 15.0 %fusion.130 = (f32[8,1024]{1,0:T(8,128)S(1)}, f32[8,1024,1024]{1,2,0:T(8,128)}) fusion(bf16[1024,8,64]{0,2,1:T(8,128)(2,1)S(1)} %bitcast.179, bf16[1024,8,64]{0,2,1:T(8,128)(2,1)S(1)} %bitcast.180), kind=kOutput, calls=%fused_computation.122 | convolution fusion | flops 1098908672 | bytes 35684352 | tf_op jit(solution)/shard_map/while/body/eval_jaxpr/sub | solution.py:25
  128.7 13.4 %fusion.112 = bf16[8,64,1024]{2,1,0:T(8,128)(2,1)} fusion(bf16[1024,8,64]{0,2,1:T(8,128)(2,1)S(1)} %bitcast.178, f32[8,1024,1024]{1,2,0:T(8,128)} %get-tuple-element.35, f32[8,1024]{1,0:T(8,128)S(1)} %get-tuple-element.34), kind=kOutput, calls=%fused_computation.100 | convolution fusion | flops 1091043328 | bytes 35684352 | tf_op jit(solution)/shard_map/while/body/eval_jaxpr/ghlm,gmhd->glhd/dot_general | solution.py:26
  142.1 2.5 copy.53
  144.7 3.8 all-to-all-start
  149.4 100.7 %all-to-all-done = bf16[512,4,512]{0,2,1:T(8,128)(2,1)S(1)} async-done(((bf16[512,4,512]{0,2,1:T(8,128)(2,1)}), bf16[512,4,512]{0,2,1:T(8,128)(2,1)S(1)}, u32[]{:S(2)}, u32[]{:S(2)}) %all-to-all-start) | async-done | bytes 2097184 | tf_op jit(solution)/shard_map/all_to_all | solution.py:69
  250.1 2.4 copy.54
  252.5 12.0 %all-gather.7.cloned.1.call-done = bf16[1,1024,2048]{1,2,0:T(8,128)(2,1)} async-done(((bf16[1,1024,512]{1,2,0:T(8,128)(2,1)}), bf16[1,1024,2048]{1,2,0:T(8,128)(2,1)}) %all-gather.7.cloned.1.call-update) | async-done | bytes 4194320 | tf_op jit(solution)/shard_map/all_gather | solution.py:70
  264.5 6.2 fusion.75
  270.8 79.9 %all-gather.9.cloned.1.call-done = bf16[1,1024,2048]{2,1,0:T(8,128)(2,1)} async-done(((bf16[1,1024,512]{2,1,0:T(8,128)(2,1)}), bf16[1,1024,2048]{2,1,0:T(8,128)(2,1)}) %all-gather.9.cloned.1.call-update) | async-done | bytes 4194320 | tf_op jit(solution)/shard_map/all_gather | solution.py:72
  350.6 3.0 convert_reduce_fusion.1
  355.3 2.0 fusion.42
  357.6 2.3 fusion.113
  359.9 2.3 fusion.116
  362.2 2.3 fusion.119
  364.9 2.7 copy.56
  367.6 52.7 %all_to_all.59 = bf16[1,1024,3,512]{3,2,0,1:T(4,128)(2,1)S(1)} all-to-all(bf16[1,1024,3,512]{3,2,0,1:T(4,128)(2,1)S(1)} %copy.56), channel_id=1, replica_groups=mesh['seq'=8,'head'=4] {'seq'}, dimensions={1} | all-to-all | bytes 6291456 | tf_op jit(solution)/shard_map/all_to_all | solution.py:76
  423.3 3.0 copy.63
  426.3 1.6 copy.60
  427.9 3.8 copy.61
  431.7 2.8 fusion.65
  434.6 4.6 fusion.131
  439.9 3.0 copy.59
  442.9 4.3 convert_bitcast_fusion
  447.1 3.3 copy.65
  450.4 1.8 copy.66
  452.2 1.6 copy.75
  454.4 7.0 reduce.19
  461.4 1.6 reshape.389
  463.0 3.6 all-to-all-start.1
  466.6 1.6 copy.74
  468.2 13.7 %all-to-all-done.1 = bf16[8,2,32768]{2,1,0:T(2,128)(2,1)S(1)} async-done(((bf16[8,2,32768]{2,1,0:T(2,128)(2,1)}), bf16[8,2,32768]{2,1,0:T(2,128)(2,1)S(1)}, u32[]{:S(2)}, u32[]{:S(2)}) %all-to-all-start.1) | async-done | bytes 1048608 | tf_op jit(solution)/shard_map/all_to_all | solution.py:77
  481.9 4.5 all-to-all-start.3
  487.5 1.6 copy.70
  489.1 85.1 %all-to-all-done.3 = bf16[512,4,512]{2,0,1:T(8,128)(2,1)} async-done(((bf16[512,4,512]{2,0,1:T(8,128)(2,1)}), bf16[512,4,512]{2,0,1:T(8,128)(2,1)}, u32[]{:S(2)}, u32[]{:S(2)}) %all-to-all-start.3) | async-done | bytes 2097184 | tf_op jit(solution)/shard_map/all_to_all | solution.py:88
  574.2 6.8 add_convert_fusion.1
  581.2 79.1 %all-gather.13.cloned.1.call-done = bf16[8,128,2048]{2,1,0:T(8,128)(2,1)} async-done(((bf16[8,128,512]{2,1,0:T(8,128)(2,1)}), bf16[8,128,2048]{2,1,0:T(8,128)(2,1)}) %all-gather.13.cloned.1.call-update) | async-done | bytes 4194320 | tf_op jit(solution)/shard_map/all_gather | solution.py:93
  660.3 3.0 convert_reduce_fusion
  665.0 27.8 %fusion.29 = f32[8,128,2048]{2,1,0:T(8,128)} fusion(bf16[2048,2048]{1,0:T(8,128)(2,1)} %param.15, bf16[2048,2048]{1,0:T(8,128)(2,1)} %param.14, bf16[8,128,2048]{2,1,0:T(8,128)(2,1)} %all-gather.13.cloned.1.call-done, f32[2048]{0:T(1024)S(1)} %bitcast.171, f32[2048]{0:T(1024)S(1)} %bitcast.170, f32[8,128]{1,0:T(8,128)S(1)} %add_rsqrt_fusion, ...), kind=kOutput, calls=%fused_computation.36 | convolution fusion | flops 17211326464 | bytes 29384704 | tf_op jit(solution)/shard_map/dot_general | solution.py:97
  692.8 143.3 %reduce-scatter.2.cloned.1.call-done = f32[8,128,512]{2,1,0:T(8,128)} async-done(((f32[8,128,2048]{2,1,0:T(8,128)}), f32[8,128,512]{2,1,0:T(8,128)}) %reduce-scatter.2.cloned.1.call-update) | async-done | bytes 2097168 | tf_op jit(solution)/shard_map/reduce_scatter | solution.py:98
  836.1 2.9 add_convert_fusion
  (65 shorter events, 14.2 us)
Async XLA Ops:
  6.5 85.9 %all-gather.15.cloned.1.call-start = ((), (), s32[]{:S(2)}) async-start(), calls=%async_computation.10 | async-start | bytes 5242880 | tf_op jit(solution)/shard_map/all_gather | solution.py:56
  7.3 257.2 %all-gather.7.cloned.1.call-start = ((), (), s32[]{:S(2)}) async-start(), calls=%async_computation.5 | async-start | bytes 5242880 | tf_op jit(solution)/shard_map/all_gather | solution.py:70
  98.7 3.4 copy-start
  103.2 2.6 slice-start
  104.2 2.2 slice-start.1
  128.7 13.4 %copy-start.6 = (bf16[512,2048]{1,0:T(8,128)(2,1)S(1)}, bf16[512,2048]{1,0:T(8,128)(2,1)}, u32[]{:S(2)}) copy-start(bf16[512,2048]{1,0:T(8,128)(2,1)} %param.11) | copy-start | bytes 6291460
  144.7 119.8 %copy-start.8 = (bf16[1,1024,512]{2,1,0:T(8,128)(2,1)S(1)}, bf16[1,1024,512]{2,1,0:T(8,128)(2,1)}, u32[]{:S(2)}) copy-start(bf16[1,1024,512]{2,1,0:T(8,128)(2,1)} %param.8) | copy-start | bytes 3145732
  144.7 105.4 %all-to-all-start = ((bf16[512,4,512]{0,2,1:T(8,128)(2,1)}), bf16[512,4,512]{0,2,1:T(8,128)(2,1)S(1)}, u32[]{:S(2)}, u32[]{:S(2)}) async-start(bf16[512,4,512]{0,2,1:T(8,128)(2,1)} %bitcast.153), calls=%async_computation | async-start | bytes 4194304 | tf_op jit(solution)/shard_map/all_to_all | solution.py:69
  148.4 202.2 %all-gather.9.cloned.1.call-start = ((), (), s32[]{:S(2)}) async-start(), calls=%async_computation.6 | async-start | bytes 5242880 | tf_op jit(solution)/shard_map/all_gather | solution.py:72
  270.7 303.5 %all-gather.11.cloned.1.call-start = ((), (), s32[]{:S(2)}) async-start(), calls=%async_computation.7 | async-start | bytes 5242880 | tf_op jit(solution)/shard_map/all_gather | solution.py:89
  350.6 3.4 copy-start.1
  354.1 3.3 slice-start.2
  355.3 2.3 slice-start.3
  434.5 4.7 copy-start.5
  447.1 5.1 copy-start.3
  461.4 5.2 copy-start.7
  463.0 18.9 %all-to-all-start.1 = ((bf16[8,2,32768]{2,1,0:T(2,128)(2,1)}), bf16[8,2,32768]{2,1,0:T(2,128)(2,1)S(1)}, u32[]{:S(2)}, u32[]{:S(2)}) async-start(bf16[8,2,32768]{2,1,0:T(2,128)(2,1)} %reshape.389), calls=%async_computation.1 | async-start | bytes 2097152 | tf_op jit(solution)/shard_map/all_to_all | solution.py:77
  481.9 92.3 %all-to-all-start.3 = ((bf16[512,4,512]{2,0,1:T(8,128)(2,1)}), bf16[512,4,512]{2,0,1:T(8,128)(2,1)}, u32[]{:S(2)}, u32[]{:S(2)}) async-start(bf16[512,4,512]{2,0,1:T(8,128)(2,1)} %bitcast.147), calls=%async_computation.3 | async-start | bytes 4194304 | tf_op jit(solution)/shard_map/all_to_all | solution.py:88
  486.4 173.9 %all-gather.13.cloned.1.call-start = ((), (), s32[]{:S(2)}) async-start(), calls=%async_computation.8 | async-start | bytes 5242880 | tf_op jit(solution)/shard_map/all_gather | solution.py:93
  581.0 84.0 %copy-start.10 = (f32[1,2048]{1,0:T(1,128)S(1)}, f32[1,2048]{1,0:T(1,128)}, u32[]{:S(2)}) copy-start(f32[1,2048]{1,0:T(1,128)} %get-tuple-element.33) | copy-start | bytes 24580
  581.0 84.0 %copy-start.9 = (f32[1,2048]{1,0:T(1,128)S(1)}, f32[1,2048]{1,0:T(1,128)}, u32[]{:S(2)}) copy-start(f32[1,2048]{1,0:T(1,128)} %get-tuple-element.28) | copy-start | bytes 24580
  581.0 255.1 %reduce-scatter.2.cloned.1.call-start = ((), (), s32[]{:S(2)}) async-start(), calls=%async_computation.9 | async-start | bytes 10485760 | tf_op jit(solution)/shard_map/reduce_scatter | solution.py:98
  660.3 3.4 copy-start.2
  692.8 143.3 %copy-start.4 = (bf16[8,128,512]{2,1,0:T(8,128)(2,1)S(1)}, bf16[8,128,512]{2,1,0:T(8,128)(2,1)}, u32[]{:S(2)}) copy-start(bf16[8,128,512]{2,1,0:T(8,128)(2,1)} %add_convert_fusion.1) | copy-start | bytes 3145732
Sparse Core Ops, SparseCore 0:
  8.9 83.4 all-gather.14
  142.3 122.1 all-gather.6
  270.8 79.7 all-gather.8
  452.4 121.0 all-gather.10
  581.1 79.1 all-gather.12
  692.9 143.0 reduce-scatter.1
